TPU v7x, 32 devices: a whole 2x2x4 slice. The times are simulated.
32 devices in a mesh: clients: 8 (over z, x), shard: 4 (over y, core).
Axes of the slice: x: 2, y: 2, z: 4, core: 2. Of those that a mesh axis runs over, the one named last changes fastest.
Arguments:
- quantized: int32 [8, 2097152], P('clients', 'shard'), may hold values from 0 to 2097151
- pair_masks: int32 [8, 2097152], P('clients', 'shard'), may hold values from 0 to 2097142, as said below
- alive_flags: int32 [8], P('clients'), may hold values from 0 to 1, as said below
- row_seeds: int32 [64], replicated, may hold values from 0 to 1073741823
Outputs:
- aggregate: int32 [2097152], P('shard')
- commitments: int32 [8, 64], P('clients')
- mismatch: int32 [64], replicated
Inputs may be any that keep to these rules, and one draw needn't show every extreme that they name: For every position, the pair_masks of all 8 participants sum to a multiple of 2097143. `alive_flags`: at least one participant has flag 1 and at least one has flag 0.
All inputs are finite; a program needn't handle non-finite values.
Results may differ from a plain program's by a relative error of at most 0.000001.
Values may be sent and summed in bfloat16 or wider, within the bound.
A program may use at most 64 MiB of HBM per device.

v0:
```python
import math
import jax
import jax.numpy as jnp
from jax import lax
from jax.sharding import PartitionSpec as P

modulus = 2097143


def table_entries(row_seeds, columns):
    mixed = columns[None, :] * 747796405 + row_seeds[:, None]
    mixed = mixed & 2147483647
    mixed = mixed ^ mixed >> 15
    mixed = mixed * 277803737 & 2147483647
    mixed = mixed ^ mixed >> 13
    mixed = mixed * 1103515245 & 2147483647
    mixed = mixed ^ mixed >> 16
    return mixed & 1023


def project_mod(row_seeds, vectors, offset, block_width):
    vec_count = vectors.shape[0]
    length = vectors.shape[1]
    row_count = row_seeds.shape[0]
    sub_width = math.gcd(block_width, 512)
    block_count = length // block_width

    def advance(running, block_index):
        start_col = block_index * block_width
        columns = offset + start_col + jnp.arange(block_width, dtype=jnp.int32)
        table = table_entries(row_seeds, columns)
        right_part = lax.dynamic_slice_in_dim(vectors, start_col, block_width, 1)
        products = right_part[:, None, :] * table[None, :, :] % modulus
        products = products.reshape(vec_count, row_count, block_width // sub_width, sub_width)
        partial_value = jnp.sum(products, axis=3, dtype=jnp.int32) % modulus
        partial_value = jnp.sum(partial_value, axis=2, dtype=jnp.int32) % modulus
        return ((running + partial_value) % modulus, None)

    running = jnp.zeros((vec_count, row_count), jnp.int32)
    running, unused = lax.scan(advance, running, jnp.arange(block_count, dtype=jnp.int32))
    return running


def block_size(length):
    return length // 16


def body(quantized, pair_masks, alive_flags, row_seeds):
    alive_now = alive_flags[0]
    length = quantized.shape[1]
    masked = (quantized[0] + pair_masks[0]) % modulus * alive_now
    share_length = length // lax.axis_size("clients")
    client_index = lax.axis_index("clients")
    summed = lax.psum(masked, "clients")
    aggregate = summed % modulus
    share_piece = lax.dynamic_slice_in_dim(aggregate, client_index * share_length, share_length, 0)
    offset = lax.axis_index("shard") * length
    own_part = project_mod(row_seeds, quantized, offset, block_size(length))[0]
    own_total = lax.psum(own_part, "shard") % modulus
    commitments = own_total[None, :]
    piece_start = offset + client_index * share_length
    projected_part = project_mod(
        row_seeds, share_piece[None, :], piece_start, block_size(share_length)
    )[0]
    weighted = own_total * alive_now
    projected = lax.psum(projected_part, ("clients", "shard")) % modulus
    expected = lax.psum(weighted, "clients") % modulus
    mismatch = (projected - expected) % modulus
    return (aggregate, commitments, mismatch)


def solution(mesh):
    placed = (P("clients", "shard"), P("clients", "shard"), P("clients"), P())
    return jax.shard_map(
        body,
        mesh=mesh,
        in_specs=placed,
        out_specs=(P("shard"), P("clients", None), P()),
        check_vma=False,
    )
```

profile of v0, /device:TPU:0, one launch (start us, length us, event | category | flops | bytes accessed | tf_op | source)
XLA Modules:
  0.0 342.2 jit_solution(15196851076049243759)
XLA Ops:
  7.9 10.4 %add_remainder_fusion = s32[1,524288]{1,0:T(1,128)S(1)} fusion(s32[1,524288]{1,0:T(1,128)} %param.8, s32[1,524288]{1,0:T(1,128)} %param.9), kind=kLoop, calls=%fused_computation.43 | loop fusion | flops 1048576 | bytes 6291456 | tf_op jit(solution)/shard_map/jit(remainder)/rem | solution.py:51
  18.3 1.7 fusion.20
  20.6 206.8 %while.26 = (s32[]{:T(128)}, s32[1,64]{1,0:T(1,128)S(1)}, s32[16]{0:T(128)S(1)}, s32[1,524288]{1,0:T(1,128)}, s32[]{:T(128)}, /*index=5*/s32[64]{0:T(128)S(1)}, s32[]{:T(128)}, s32[1]{0:T(128)}, s32[]{:T(128)}, s32[]{:T(128)}) while((s32[]{:T(128)}, s32[1,64]{1,0:T(1,128)S(1)}, s32[16]{0:T(128)S(1)}, s32[1,524288]{1,0:T(1,128)}, ...), condition=%wide.region_4.5_spmd.clone, body=%wide.region_1.4_spmd.clone.sunk | while | flops 44196680 | bytes 951749 | solution.py:40
  21.9 1.2 dynamic-slice_reduce_fusion.4
  23.1 10.3 %fusion.27 = s32[64,64]{1,0:T(8,128)S(1)} fusion(s32[64]{0:T(128)S(1)} %get-tuple-element.328, s32[64,512]{1,0:T(8,128)S(1)} %add_multiply_fusion.4, s32[64,512]{1,0:T(8,128)S(1)} %mul.283), kind=kLoop, calls=%fused_computation.11.clone.1 | loop fusion | flops 44036096 | bytes 278784 | tf_op jit(solution)/shard_map/while/body/eval_jaxpr/reduce_sum | solution.py:35
  34.8 1.2 dynamic-slice_reduce_fusion.4
  36.0 10.3 %fusion.27 = s32[64,64]{1,0:T(8,128)S(1)} fusion(s32[64]{0:T(128)S(1)} %get-tuple-element.328, s32[64,512]{1,0:T(8,128)S(1)} %add_multiply_fusion.4, s32[64,512]{1,0:T(8,128)S(1)} %mul.283), kind=kLoop, calls=%fused_computation.11.clone.1 | loop fusion | flops 44036096 | bytes 278784 | tf_op jit(solution)/shard_map/while/body/eval_jaxpr/reduce_sum | solution.py:35
  47.8 1.2 dynamic-slice_reduce_fusion.4
  48.9 10.3 %fusion.27 = s32[64,64]{1,0:T(8,128)S(1)} fusion(s32[64]{0:T(128)S(1)} %get-tuple-element.328, s32[64,512]{1,0:T(8,128)S(1)} %add_multiply_fusion.4, s32[64,512]{1,0:T(8,128)S(1)} %mul.283), kind=kLoop, calls=%fused_computation.11.clone.1 | loop fusion | flops 44036096 | bytes 278784 | tf_op jit(solution)/shard_map/while/body/eval_jaxpr/reduce_sum | solution.py:35
  61.9 10.3 %fusion.27 = s32[64,64]{1,0:T(8,128)S(1)} fusion(s32[64]{0:T(128)S(1)} %get-tuple-element.328, s32[64,512]{1,0:T(8,128)S(1)} %add_multiply_fusion.4, s32[64,512]{1,0:T(8,128)S(1)} %mul.283), kind=kLoop, calls=%fused_computation.11.clone.1 | loop fusion | flops 44036096 | bytes 278784 | tf_op jit(solution)/shard_map/while/body/eval_jaxpr/reduce_sum | solution.py:35
  73.6 1.2 dynamic-slice_reduce_fusion.4
  74.8 10.3 %fusion.27 = s32[64,64]{1,0:T(8,128)S(1)} fusion(s32[64]{0:T(128)S(1)} %get-tuple-element.328, s32[64,512]{1,0:T(8,128)S(1)} %add_multiply_fusion.4, s32[64,512]{1,0:T(8,128)S(1)} %mul.283), kind=kLoop, calls=%fused_computation.11.clone.1 | loop fusion | flops 44036096 | bytes 278784 | tf_op jit(solution)/shard_map/while/body/eval_jaxpr/reduce_sum | solution.py:35
  86.5 1.2 dynamic-slice_reduce_fusion.4
  87.7 10.3 %fusion.27 = s32[64,64]{1,0:T(8,128)S(1)} fusion(s32[64]{0:T(128)S(1)} %get-tuple-element.328, s32[64,512]{1,0:T(8,128)S(1)} %add_multiply_fusion.4, s32[64,512]{1,0:T(8,128)S(1)} %mul.283), kind=kLoop, calls=%fused_computation.11.clone.1 | loop fusion | flops 44036096 | bytes 278784 | tf_op jit(solution)/shard_map/while/body/eval_jaxpr/reduce_sum | solution.py:35
  99.5 1.2 dynamic-slice_reduce_fusion.4
  100.7 10.3 %fusion.27 = s32[64,64]{1,0:T(8,128)S(1)} fusion(s32[64]{0:T(128)S(1)} %get-tuple-element.328, s32[64,512]{1,0:T(8,128)S(1)} %add_multiply_fusion.4, s32[64,512]{1,0:T(8,128)S(1)} %mul.283), kind=kLoop, calls=%fused_computation.11.clone.1 | loop fusion | flops 44036096 | bytes 278784 | tf_op jit(solution)/shard_map/while/body/eval_jaxpr/reduce_sum | solution.py:35
  112.4 1.2 dynamic-slice_reduce_fusion.4
  113.6 10.3 %fusion.27 = s32[64,64]{1,0:T(8,128)S(1)} fusion(s32[64]{0:T(128)S(1)} %get-tuple-element.328, s32[64,512]{1,0:T(8,128)S(1)} %add_multiply_fusion.4, s32[64,512]{1,0:T(8,128)S(1)} %mul.283), kind=kLoop, calls=%fused_computation.11.clone.1 | loop fusion | flops 44036096 | bytes 278784 | tf_op jit(solution)/shard_map/while/body/eval_jaxpr/reduce_sum | solution.py:35
  125.3 1.2 dynamic-slice_reduce_fusion.4
  126.5 10.3 %fusion.27 = s32[64,64]{1,0:T(8,128)S(1)} fusion(s32[64]{0:T(128)S(1)} %get-tuple-element.328, s32[64,512]{1,0:T(8,128)S(1)} %add_multiply_fusion.4, s32[64,512]{1,0:T(8,128)S(1)} %mul.283), kind=kLoop, calls=%fused_computation.11.clone.1 | loop fusion | flops 44036096 | bytes 278784 | tf_op jit(solution)/shard_map/while/body/eval_jaxpr/reduce_sum | solution.py:35
  139.4 10.3 %fusion.27 = s32[64,64]{1,0:T(8,128)S(1)} fusion(s32[64]{0:T(128)S(1)} %get-tuple-element.328, s32[64,512]{1,0:T(8,128)S(1)} %add_multiply_fusion.4, s32[64,512]{1,0:T(8,128)S(1)} %mul.283), kind=kLoop, calls=%fused_computation.11.clone.1 | loop fusion | flops 44036096 | bytes 278784 | tf_op jit(solution)/shard_map/while/body/eval_jaxpr/reduce_sum | solution.py:35
  152.3 10.3 %fusion.27 = s32[64,64]{1,0:T(8,128)S(1)} fusion(s32[64]{0:T(128)S(1)} %get-tuple-element.328, s32[64,512]{1,0:T(8,128)S(1)} %add_multiply_fusion.4, s32[64,512]{1,0:T(8,128)S(1)} %mul.283), kind=kLoop, calls=%fused_computation.11.clone.1 | loop fusion | flops 44036096 | bytes 278784 | tf_op jit(solution)/shard_map/while/body/eval_jaxpr/reduce_sum | solution.py:35
  165.3 10.3 %fusion.27 = s32[64,64]{1,0:T(8,128)S(1)} fusion(s32[64]{0:T(128)S(1)} %get-tuple-element.328, s32[64,512]{1,0:T(8,128)S(1)} %add_multiply_fusion.4, s32[64,512]{1,0:T(8,128)S(1)} %mul.283), kind=kLoop, calls=%fused_computation.11.clone.1 | loop fusion | flops 44036096 | bytes 278784 | tf_op jit(solution)/shard_map/while/body/eval_jaxpr/reduce_sum | solution.py:35
  178.2 10.3 %fusion.27 = s32[64,64]{1,0:T(8,128)S(1)} fusion(s32[64]{0:T(128)S(1)} %get-tuple-element.328, s32[64,512]{1,0:T(8,128)S(1)} %add_multiply_fusion.4, s32[64,512]{1,0:T(8,128)S(1)} %mul.283), kind=kLoop, calls=%fused_computation.11.clone.1 | loop fusion | flops 44036096 | bytes 278784 | tf_op jit(solution)/shard_map/while/body/eval_jaxpr/reduce_sum | solution.py:35
  191.1 10.3 %fusion.27 = s32[64,64]{1,0:T(8,128)S(1)} fusion(s32[64]{0:T(128)S(1)} %get-tuple-element.328, s32[64,512]{1,0:T(8,128)S(1)} %add_multiply_fusion.4, s32[64,512]{1,0:T(8,128)S(1)} %mul.283), kind=kLoop, calls=%fused_computation.11.clone.1 | loop fusion | flops 44036096 | bytes 278784 | tf_op jit(solution)/shard_map/while/body/eval_jaxpr/reduce_sum | solution.py:35
  204.0 10.3 %fusion.27 = s32[64,64]{1,0:T(8,128)S(1)} fusion(s32[64]{0:T(128)S(1)} %get-tuple-element.328, s32[64,512]{1,0:T(8,128)S(1)} %add_multiply_fusion.4, s32[64,512]{1,0:T(8,128)S(1)} %mul.283), kind=kLoop, calls=%fused_computation.11.clone.1 | loop fusion | flops 44036096 | bytes 278784 | tf_op jit(solution)/shard_map/while/body/eval_jaxpr/reduce_sum | solution.py:35
  217.0 10.3 %fusion.27 = s32[64,64]{1,0:T(8,128)S(1)} fusion(s32[64]{0:T(128)S(1)} %get-tuple-element.328, s32[64,512]{1,0:T(8,128)S(1)} %add_multiply_fusion.4, s32[64,512]{1,0:T(8,128)S(1)} %mul.283), kind=kLoop, calls=%fused_computation.11.clone.1 | loop fusion | flops 44036096 | bytes 278784 | tf_op jit(solution)/shard_map/while/body/eval_jaxpr/reduce_sum | solution.py:35
  227.4 6.4 %psum.29 = s32[64]{0:T(128)S(1)} all-reduce(s32[64]{0:T(128)S(1)} %bitcast.30), channel_id=1, replica_groups=mesh['clients'=8,'shard'=4] {'shard'}, use_global_device_ids=true, to_apply=%region_5.6 | all-reduce | flops 64 | bytes 512 | tf_op jit(solution)/shard_map/psum | solution.py:59
  234.4 11.6 %psum.31 = s32[64]{0:T(128)S(1)} all-reduce(s32[64]{0:T(128)S(1)} %get-tuple-element.227), channel_id=1, replica_groups=mesh['clients'=8,'shard'=4] {'clients'}, use_global_device_ids=true, to_apply=%region_11.12 | all-reduce | flops 64 | bytes 512 | tf_op jit(solution)/shard_map/psum | solution.py:67
  246.0 2.5 add_select_fusion.4
  248.5 47.8 %while.27 = (s32[]{:T(128)}, s32[1,64]{1,0:T(1,128)S(1)}, s32[16]{0:T(128)S(1)}, s32[1,65536]{1,0:T(1,128)S(1)}, s32[]{:T(128)}, /*index=5*/s32[64]{0:T(128)S(1)}, s32[]{:T(128)}, s32[1]{0:T(128)}, s32[]{:T(128)}, s32[]{:T(128)}) while((s32[]{:T(128)}, s32[1,64]{1,0:T(1,128)S(1)}, s32[16]{0:T(128)S(1)}, s32[1,65536]{1,0:T(1,128)S(1)}, ...), condition=%wide.region_9.10_spmd.clone, body=%wide.region_6.9_spmd.clone.sunk | while | flops 5525320 | bytes 120261 | solution.py:40
  250.0 1.5 fusion.29
  253.0 1.5 fusion.29
  256.0 1.5 fusion.29
  258.9 1.5 fusion.29
  261.9 1.5 fusion.29
  264.9 1.5 fusion.29
  267.9 1.5 fusion.29
  270.9 1.5 fusion.29
  273.8 1.5 fusion.29
  276.8 1.5 fusion.29
  279.8 1.5 fusion.29
  282.8 1.5 fusion.29
  285.8 1.5 fusion.29
  288.7 1.5 fusion.29
  291.7 1.5 fusion.29
  294.7 1.5 fusion.29
  296.4 38.5 %psum.30 = s32[64]{0:T(128)S(1)} all-reduce(s32[64]{0:T(128)S(1)} %bitcast.29), channel_id=1, replica_groups=mesh['clients'=8,'shard'=4] {'clients','shard'}, use_global_device_ids=true, to_apply=%region_10.11 | all-reduce | flops 64 | bytes 512 | tf_op jit(solution)/shard_map/psum | solution.py:66
  (198 shorter events, 37.0 us)
Async XLA Ops:
  7.2 238.8 %all-reduce.2.cloned.1.call-start = ((), (), s32[]{:S(2)}) async-start(), calls=%async_computation | async-start | bytes 4194304 | tf_op jit(solution)/shard_map/psum | solution.py:54
  20.0 0.7 copy-start.1
  248.5 86.9 %copy-start = (s32[524288]{0:T(1024)}, s32[524288]{0:T(1024)S(1)}, u32[]{:S(2)}) copy-start(s32[524288]{0:T(1024)S(1)} %add_select_fusion.4) | copy-start | bytes 6291460
Sparse Core Ops, SparseCore 0:
  20.1 105.0 all-reduce.1
where the time goes:
time: 343 us; the launch traced here: 342 us
  other arithmetic  210 us (61%)
  blocking collectives  56.5 us (16%)
  local copies, waits for them, and re-layouts  39.6 us (12%)
  loops' own time  21.8 us (6%)
  between operations  14.8 us (4%)
    reduce_sum x32, other arithmetic, advance(): partial_value = jnp.sum(products, axis=3, dtype=jnp.int32) % modulus  188 us
    psum x1, blocking collectives, body(): projected = lax.psum(projected_part, ('clients', 'shard')) % modulus  38.5 us
    another operation x2, loops' own time, project_mod(): lax.scan(advance, running, jnp.arange(block_count, dtype=jnp.int32))  21.8 us
    dynamic_slice x32, local copies, waits for them, and re-layouts, project_mod(): lax.scan(advance, running, jnp.arange(block_count, dtype=jnp.int32))  19.4 us
    dynamic_slice x32, local copies, waits for them, and re-layouts, advance(): right_part = lax.dynamic_slice_in_dim(vectors, start_col, block_width, 1)  19.1 us
    psum x1, blocking collectives, body(): expected = lax.psum(weighted, 'clients') % modulus  11.6 us
    rem x1, other arithmetic, body(): masked = (quantized[0] + pair_masks[0]) % modulus * alive_now  10.4 us
  transfers between devices with their start and end apart: 1, of which 0 were waited for; matrix products, arithmetic and copies ran while one was open for 58% of the time, Pallas kernels for 0%

commit v1 on v0

--- a/solution.py
+++ b/solution.py
@@ -63,7 +63,7 @@
         row_seeds, share_piece[None, :], piece_start, block_size(share_length)
     )[0]
     weighted = own_total * alive_now
-    projected = lax.psum(projected_part, ("clients", "shard")) % modulus
+    projected = lax.psum(lax.psum(projected_part, "shard"), "clients") % modulus
     expected = lax.psum(weighted, "clients") % modulus
     mismatch = (projected - expected) % modulus
     return (aggregate, commitments, mismatch)

time: 343 us -> 307 us (0.90)
  blocking collectives: 56.5 us -> 18 us
    psum x1 -> x0, blocking collectives: 38.5 us -> none  [body(): projected = lax.psum(projected_part, ('clients', 'shard')) % modulus]
  transfers between devices with their start and end apart: 1 -> 1, of which waited for: 0 -> 0; matrix products, arithmetic and copies ran while one was open for 58% -> 64% of each run, Pallas kernels for 0% -> 0%
where the time goes in v1:
time: 307 us; the launch traced here: 306 us
  other arithmetic  210 us (68%)
  local copies, waits for them, and re-layouts  40.9 us (13%)
  loops' own time  22.5 us (7%)
  blocking collectives  18 us (6%)
  between operations  14.8 us (5%)
    reduce_sum x32, other arithmetic, advance(): partial_value = jnp.sum(products, axis=3, dtype=jnp.int32) % modulus  188 us
    another operation x2, loops' own time, project_mod(): lax.scan(advance, running, jnp.arange(block_count, dtype=jnp.int32))  22.5 us
    dynamic_slice x32, local copies, waits for them, and re-layouts, project_mod(): lax.scan(advance, running, jnp.arange(block_count, dtype=jnp.int32))  20.7 us
    dynamic_slice x32, local copies, waits for them, and re-layouts, advance(): right_part = lax.dynamic_slice_in_dim(vectors, start_col, block_width, 1)  19.1 us
    psum x1, blocking collectives, body(): expected = lax.psum(weighted, 'clients') % modulus  11.6 us
    rem x1, other arithmetic, body(): masked = (quantized[0] + pair_masks[0]) % modulus * alive_now  10.4 us
    psum x1, blocking collectives, body(): own_total = lax.psum(own_part, 'shard') % modulus  6.44 us
  transfers between devices with their start and end apart: 1, of which 0 were waited for; matrix products, arithmetic and copies ran while one was open for 64% of the time, Pallas kernels for 0%

profile of v1, /device:TPU:0, one launch (start us, length us, event | category | flops | bytes accessed | tf_op | source)
XLA Modules:
  0.0 305.8 jit_solution(6449962929685932060)
XLA Ops:
  7.9 10.4 %add_remainder_fusion = s32[1,524288]{1,0:T(1,128)S(1)} fusion(s32[1,524288]{1,0:T(1,128)} %param.8, s32[1,524288]{1,0:T(1,128)} %param.9), kind=kLoop, calls=%fused_computation.43 | loop fusion | flops 1048576 | bytes 6291456 | tf_op jit(solution)/shard_map/jit(remainder)/rem | solution.py:51
  18.3 1.7 fusion.20
  20.6 206.8 %while.26 = (s32[]{:T(128)}, s32[1,64]{1,0:T(1,128)S(1)}, s32[16]{0:T(128)S(1)}, s32[1,524288]{1,0:T(1,128)}, s32[]{:T(128)}, /*index=5*/s32[64]{0:T(128)S(1)}, s32[]{:T(128)}, s32[1]{0:T(128)}, s32[]{:T(128)}, s32[]{:T(128)}) while((s32[]{:T(128)}, s32[1,64]{1,0:T(1,128)S(1)}, s32[16]{0:T(128)S(1)}, s32[1,524288]{1,0:T(1,128)}, ...), condition=%wide.region_4.5_spmd.clone, body=%wide.region_1.4_spmd.clone.sunk | while | flops 44196680 | bytes 951749 | solution.py:40
  21.9 1.2 dynamic-slice_reduce_fusion.4
  23.1 10.3 %fusion.27 = s32[64,64]{1,0:T(8,128)S(1)} fusion(s32[64]{0:T(128)S(1)} %get-tuple-element.332, s32[64,512]{1,0:T(8,128)S(1)} %add_multiply_fusion.4, s32[64,512]{1,0:T(8,128)S(1)} %mul.283), kind=kLoop, calls=%fused_computation.11.clone.1 | loop fusion | flops 44036096 | bytes 278784 | tf_op jit(solution)/shard_map/while/body/eval_jaxpr/reduce_sum | solution.py:35
  34.8 1.2 dynamic-slice_reduce_fusion.4
  36.0 10.3 %fusion.27 = s32[64,64]{1,0:T(8,128)S(1)} fusion(s32[64]{0:T(128)S(1)} %get-tuple-element.332, s32[64,512]{1,0:T(8,128)S(1)} %add_multiply_fusion.4, s32[64,512]{1,0:T(8,128)S(1)} %mul.283), kind=kLoop, calls=%fused_computation.11.clone.1 | loop fusion | flops 44036096 | bytes 278784 | tf_op jit(solution)/shard_map/while/body/eval_jaxpr/reduce_sum | solution.py:35
  47.8 1.2 dynamic-slice_reduce_fusion.4
  48.9 10.3 %fusion.27 = s32[64,64]{1,0:T(8,128)S(1)} fusion(s32[64]{0:T(128)S(1)} %get-tuple-element.332, s32[64,512]{1,0:T(8,128)S(1)} %add_multiply_fusion.4, s32[64,512]{1,0:T(8,128)S(1)} %mul.283), kind=kLoop, calls=%fused_computation.11.clone.1 | loop fusion | flops 44036096 | bytes 278784 | tf_op jit(solution)/shard_map/while/body/eval_jaxpr/reduce_sum | solution.py:35
  60.7 1.2 dynamic-slice_reduce_fusion.4
  61.9 10.3 %fusion.27 = s32[64,64]{1,0:T(8,128)S(1)} fusion(s32[64]{0:T(128)S(1)} %get-tuple-element.332, s32[64,512]{1,0:T(8,128)S(1)} %add_multiply_fusion.4, s32[64,512]{1,0:T(8,128)S(1)} %mul.283), kind=kLoop, calls=%fused_computation.11.clone.1 | loop fusion | flops 44036096 | bytes 278784 | tf_op jit(solution)/shard_map/while/body/eval_jaxpr/reduce_sum | solution.py:35
  73.6 1.2 dynamic-slice_reduce_fusion.4
  74.8 10.3 %fusion.27 = s32[64,64]{1,0:T(8,128)S(1)} fusion(s32[64]{0:T(128)S(1)} %get-tuple-element.332, s32[64,512]{1,0:T(8,128)S(1)} %add_multiply_fusion.4, s32[64,512]{1,0:T(8,128)S(1)} %mul.283), kind=kLoop, calls=%fused_computation.11.clone.1 | loop fusion | flops 44036096 | bytes 278784 | tf_op jit(solution)/shard_map/while/body/eval_jaxpr/reduce_sum | solution.py:35
  86.5 1.2 dynamic-slice_reduce_fusion.4
  87.7 10.3 %fusion.27 = s32[64,64]{1,0:T(8,128)S(1)} fusion(s32[64]{0:T(128)S(1)} %get-tuple-element.332, s32[64,512]{1,0:T(8,128)S(1)} %add_multiply_fusion.4, s32[64,512]{1,0:T(8,128)S(1)} %mul.283), kind=kLoop, calls=%fused_computation.11.clone.1 | loop fusion | flops 44036096 | bytes 278784 | tf_op jit(solution)/shard_map/while/body/eval_jaxpr/reduce_sum | solution.py:35
  99.5 1.2 dynamic-slice_reduce_fusion.4
  100.7 10.3 %fusion.27 = s32[64,64]{1,0:T(8,128)S(1)} fusion(s32[64]{0:T(128)S(1)} %get-tuple-element.332, s32[64,512]{1,0:T(8,128)S(1)} %add_multiply_fusion.4, s32[64,512]{1,0:T(8,128)S(1)} %mul.283), kind=kLoop, calls=%fused_computation.11.clone.1 | loop fusion | flops 44036096 | bytes 278784 | tf_op jit(solution)/shard_map/while/body/eval_jaxpr/reduce_sum | solution.py:35
  112.4 1.2 dynamic-slice_reduce_fusion.4
  113.6 10.3 %fusion.27 = s32[64,64]{1,0:T(8,128)S(1)} fusion(s32[64]{0:T(128)S(1)} %get-tuple-element.332, s32[64,512]{1,0:T(8,128)S(1)} %add_multiply_fusion.4, s32[64,512]{1,0:T(8,128)S(1)} %mul.283), kind=kLoop, calls=%fused_computation.11.clone.1 | loop fusion | flops 44036096 | bytes 278784 | tf_op jit(solution)/shard_map/while/body/eval_jaxpr/reduce_sum | solution.py:35
  125.3 1.2 dynamic-slice_reduce_fusion.4
  126.5 10.3 %fusion.27 = s32[64,64]{1,0:T(8,128)S(1)} fusion(s32[64]{0:T(128)S(1)} %get-tuple-element.332, s32[64,512]{1,0:T(8,128)S(1)} %add_multiply_fusion.4, s32[64,512]{1,0:T(8,128)S(1)} %mul.283), kind=kLoop, calls=%fused_computation.11.clone.1 | loop fusion | flops 44036096 | bytes 278784 | tf_op jit(solution)/shard_map/while/body/eval_jaxpr/reduce_sum | solution.py:35
  139.4 10.3 %fusion.27 = s32[64,64]{1,0:T(8,128)S(1)} fusion(s32[64]{0:T(128)S(1)} %get-tuple-element.332, s32[64,512]{1,0:T(8,128)S(1)} %add_multiply_fusion.4, s32[64,512]{1,0:T(8,128)S(1)} %mul.283), kind=kLoop, calls=%fused_computation.11.clone.1 | loop fusion | flops 44036096 | bytes 278784 | tf_op jit(solution)/shard_map/while/body/eval_jaxpr/reduce_sum | solution.py:35
  152.3 10.3 %fusion.27 = s32[64,64]{1,0:T(8,128)S(1)} fusion(s32[64]{0:T(128)S(1)} %get-tuple-element.332, s32[64,512]{1,0:T(8,128)S(1)} %add_multiply_fusion.4, s32[64,512]{1,0:T(8,128)S(1)} %mul.283), kind=kLoop, calls=%fused_computation.11.clone.1 | loop fusion | flops 44036096 | bytes 278784 | tf_op jit(solution)/shard_map/while/body/eval_jaxpr/reduce_sum | solution.py:35
  165.3 10.3 %fusion.27 = s32[64,64]{1,0:T(8,128)S(1)} fusion(s32[64]{0:T(128)S(1)} %get-tuple-element.332, s32[64,512]{1,0:T(8,128)S(1)} %add_multiply_fusion.4, s32[64,512]{1,0:T(8,128)S(1)} %mul.283), kind=kLoop, calls=%fused_computation.11.clone.1 | loop fusion | flops 44036096 | bytes 278784 | tf_op jit(solution)/shard_map/while/body/eval_jaxpr/reduce_sum | solution.py:35
  178.2 10.3 %fusion.27 = s32[64,64]{1,0:T(8,128)S(1)} fusion(s32[64]{0:T(128)S(1)} %get-tuple-element.332, s32[64,512]{1,0:T(8,128)S(1)} %add_multiply_fusion.4, s32[64,512]{1,0:T(8,128)S(1)} %mul.283), kind=kLoop, calls=%fused_computation.11.clone.1 | loop fusion | flops 44036096 | bytes 278784 | tf_op jit(solution)/shard_map/while/body/eval_jaxpr/reduce_sum | solution.py:35
  191.1 10.3 %fusion.27 = s32[64,64]{1,0:T(8,128)S(1)} fusion(s32[64]{0:T(128)S(1)} %get-tuple-element.332, s32[64,512]{1,0:T(8,128)S(1)} %add_multiply_fusion.4, s32[64,512]{1,0:T(8,128)S(1)} %mul.283), kind=kLoop, calls=%fused_computation.11.clone.1 | loop fusion | flops 44036096 | bytes 278784 | tf_op jit(solution)/shard_map/while/body/eval_jaxpr/reduce_sum | solution.py:35
  204.0 10.3 %fusion.27 = s32[64,64]{1,0:T(8,128)S(1)} fusion(s32[64]{0:T(128)S(1)} %get-tuple-element.332, s32[64,512]{1,0:T(8,128)S(1)} %add_multiply_fusion.4, s32[64,512]{1,0:T(8,128)S(1)} %mul.283), kind=kLoop, calls=%fused_computation.11.clone.1 | loop fusion | flops 44036096 | bytes 278784 | tf_op jit(solution)/shard_map/while/body/eval_jaxpr/reduce_sum | solution.py:35
  217.0 10.3 %fusion.27 = s32[64,64]{1,0:T(8,128)S(1)} fusion(s32[64]{0:T(128)S(1)} %get-tuple-element.332, s32[64,512]{1,0:T(8,128)S(1)} %add_multiply_fusion.4, s32[64,512]{1,0:T(8,128)S(1)} %mul.283), kind=kLoop, calls=%fused_computation.11.clone.1 | loop fusion | flops 44036096 | bytes 278784 | tf_op jit(solution)/shard_map/while/body/eval_jaxpr/reduce_sum | solution.py:35
  227.5 2.5 add_select_fusion.4
  230.0 49.8 %while.27 = (s32[]{:T(128)}, s32[1,64]{1,0:T(1,128)S(1)}, s32[16]{0:T(128)S(1)}, s32[1,65536]{1,0:T(1,128)S(1)}, s32[]{:T(128)}, /*index=5*/s32[64]{0:T(128)S(1)}, s32[]{:T(128)}, s32[1]{0:T(128)}, s32[]{:T(128)}, s32[]{:T(128)}) while((s32[]{:T(128)}, s32[1,64]{1,0:T(1,128)S(1)}, s32[16]{0:T(128)S(1)}, s32[1,65536]{1,0:T(1,128)S(1)}, ...), condition=%wide.region_9.10_spmd.clone, body=%wide.region_6.9_spmd.clone.sunk | while | flops 5525320 | bytes 120261 | solution.py:40
  231.6 1.5 fusion.29
  234.7 1.5 fusion.29
  237.8 1.5 fusion.29
  240.9 1.5 fusion.29
  244.0 1.5 fusion.29
  247.1 1.5 fusion.29
  250.2 1.5 fusion.29
  253.3 1.5 fusion.29
  256.4 1.5 fusion.29
  259.5 1.5 fusion.29
  262.6 1.5 fusion.29
  265.7 1.5 fusion.29
  268.9 1.5 fusion.29
  272.0 1.5 fusion.29
  275.1 1.5 fusion.29
  278.2 1.5 fusion.29
  279.8 6.4 %all-reduce.1 = (s32[64]{0:T(128)S(1)}, s32[64]{0:T(128)S(1)}) all-reduce(s32[64]{0:T(128)S(1)} %bitcast.30, s32[64]{0:T(128)S(1)} %bitcast.29), channel_id=1, replica_groups=mesh['clients'=8,'shard'=4] {'shard'}, use_global_device_ids=true, to_apply=%region_5.6 | all-reduce | flops 128 | bytes 1024 | tf_op jit(solution)/shard_map/psum | solution.py:59
  286.8 11.6 %all-reduce = (s32[64]{0:T(128)S(1)}, s32[64]{0:T(128)S(1)}) all-reduce(s32[64]{0:T(128)S(1)} %get-tuple-element.231, s32[64]{0:T(128)S(1)} %get-tuple-element.230), channel_id=1, replica_groups=mesh['clients'=8,'shard'=4] {'clients'}, use_global_device_ids=true, to_apply=%region_12.13 | all-reduce | flops 128 | bytes 1024 | tf_op jit(solution)/shard_map/psum | solution.py:67
  (197 shorter events, 37.2 us)
Async XLA Ops:
  7.2 220.3 %all-reduce.4.cloned.1.call-start = ((), (), s32[]{:S(2)}) async-start(), calls=%async_computation | async-start | bytes 4194304 | tf_op jit(solution)/shard_map/psum | solution.py:54
  20.0 0.7 copy-start.1
  230.0 69.0 %copy-start = (s32[524288]{0:T(1024)}, s32[524288]{0:T(1024)S(1)}, u32[]{:S(2)}) copy-start(s32[524288]{0:T(1024)S(1)} %add_select_fusion.4) | copy-start | bytes 6291460
Sparse Core Ops, SparseCore 0:
  20.1 105.0 all-reduce.3
